TPU v7x, 256 devices: a 8x8x2 block of a 8x8x16 slice. The times are simulated.
256 devices in a mesh: groups: 2 (over z), steps: 128 (over y, x, core).
Axes of the slice: x: 8, y: 8, z: 2, core: 2. Of those that a mesh axis runs over, the one named last changes fastest.
The devices are a block of a 8x8x16 slice.
Arguments:
- states: float32 [256, 4, 4096], P(('groups', 'steps')), parts along dimension 0, may hold values from -6 to 6
- t_sched: int32 [514], P('groups'), parts along dimension 0, may hold values from 0 to 999, as said below
- advances: int32 [4], P('groups'), parts along dimension 0, may hold values from 1 to 128, as said below
- in_weight: bfloat16 [320, 4], replicated, may hold values from -3 to 3
- time_weight: float32 [320, 320], replicated, may hold values from -0.3125 to 0.3125
- mid_weight: bfloat16 [320, 320], replicated, may hold values from -0.3125 to 0.3125
- out_weight: bfloat16 [4, 320], replicated, may hold values from -0.3125 to 0.3125
Outputs:
- final_states: float32 [256, 4, 4096], P(('groups', 'steps')), parts along dimension 0
- errors: float32 [4, 4, 128], P('groups', None, 'steps'), parts along dimension 0
There are 2 independent parts, one for each index of `groups`. A program takes and returns all parts, laid end to end along the dimension named above; an argument that names none is the same for every part. Nothing has to cross between parts.
Inputs may be any that keep to these rules, and one draw needn't show every extreme that they name: `t_sched`: strictly decreasing. Some round advances by exactly 128.
All inputs are finite; a program needn't handle non-finite values.
Results may differ from a plain program's by a relative error of at most 0.0024.
Values sent between devices are 32-bit elements; how exact they have to be, the bound alone decides.
No kernel may reach another device: no remote copies, remote signals or barrier semaphores. Data moves between devices by JAX's collectives and lax.ppermute only.
A program may use at most 64 MiB of HBM per device.

v0:
```python
import math
import jax
import jax.numpy as jnp
from jax import lax
from jax.sharding import Mesh
from jax.sharding import PartitionSpec as P

TSTEPS = 1000
ITERS = 4
ROUNDS = 2
STEPS = ("steps_0", "steps_1", "steps_2")
GROUPS_STEPS = ("groups", "steps_0", "steps_1", "steps_2")


def neutral_like(value, identity):
    return jnp.zeros_like(value) + jnp.asarray(identity, value.dtype)


def entering(value, axes, combine, identity):
    before = start = neutral_like(value, identity)
    so_far = value
    for axis in reversed(axes):
        devices, place = (lax.axis_size(axis), lax.axis_index(axis))
        pieces = lax.all_gather(so_far, axis)
        inside, so_far = (start, start)
        for k in range(devices):
            passed = k < place
            so_far = combine(so_far, pieces[k])
            inside = jnp.where(passed, so_far, inside)
        before = combine(inside, before)
    return before


def alpha_table():
    levels = jnp.arange(TSTEPS, dtype=jnp.float32)
    low = math.sqrt(0.00085)
    high = math.sqrt(0.012)
    betas = (low + (high - low) * levels / (TSTEPS - 1)) ** 2
    return jnp.exp(jnp.cumsum(jnp.log1p(-betas)))


def time_features(stamp, width):
    halfwidth = width // 2
    freqs = jnp.exp(-math.log(10000.0) * jnp.arange(halfwidth, dtype=jnp.float32) / halfwidth)
    angles = stamp.astype(jnp.float32) * freqs
    return jnp.concatenate([jnp.cos(angles), jnp.sin(angles)])


def lookup(alphas, stamp):
    levels = jnp.arange(alphas.shape[0], dtype=jnp.int32)
    return jnp.sum(jnp.where(levels == stamp, alphas, 0.0))


def denoise(state, embed, in_weight, mid_weight, out_weight):
    pre = (
        jnp.dot(in_weight, state.astype(jnp.bfloat16), preferred_element_type=jnp.float32)
        + embed[:, None]
    )
    hidden_one = jax.nn.silu(pre).astype(jnp.bfloat16)
    mixed = jnp.dot(mid_weight, hidden_one, preferred_element_type=jnp.float32)
    hidden_two = (jax.nn.silu(mixed) + pre).astype(jnp.bfloat16)
    return jnp.dot(out_weight, hidden_two, preferred_element_type=jnp.float32)


def add_terms(earlier, later):
    return earlier + later


def shards(states, t_sched, advances, in_weight, time_weight, mid_weight, out_weight):
    window = lax.axis_size(STEPS)
    own_index = lax.axis_index(STEPS)
    alphas = alpha_table()
    current = states
    window_start = jnp.int32(0)
    error_rows = []
    for round_no in range(ROUNDS):
        stamp_now = lax.dynamic_slice_in_dim(t_sched, window_start + own_index, 1)[0]
        stamp_next = lax.dynamic_slice_in_dim(t_sched, window_start + own_index + 1, 1)[0]
        alpha_now = lookup(alphas, stamp_now)
        alpha_next = lookup(alphas, stamp_next)
        coef_one = jnp.sqrt(alpha_next / alpha_now)
        coef_two = jnp.sqrt(1.0 - alpha_next) - coef_one * jnp.sqrt(1.0 - alpha_now)
        feats = time_features(stamp_now, time_weight.shape[1])
        embed = jnp.dot(time_weight, feats, precision=lax.Precision.HIGHEST)
        is_first = own_index == 0
        sweep_rows = []
        for sweep in range(ITERS):
            noise = denoise(current[0], embed, in_weight, mid_weight, out_weight)
            drift = (coef_one - 1.0) * current + coef_two * noise[None]
            term = drift + jnp.where(is_first, current, 0.0)
            prefix = entering(term, STEPS, add_terms, jnp.zeros_like(term))
            updated = jnp.where(is_first, current, prefix)
            sweep_rows.append(jnp.mean((updated - current) ** 2))
            current = updated
        error_rows.append(jnp.stack(sweep_rows))
        advance = advances[round_no]
        target = own_index + advance
        wanted = jnp.minimum(target, window - 1)
        block = lax.all_gather(current, STEPS, axis=0, tiled=True)
        row_ids = jnp.arange(block.shape[0], dtype=jnp.int32)
        selected = jnp.where((row_ids == wanted)[:, None, None], block, 0.0)
        current = jnp.zeros_like(current) + jnp.sum(selected, axis=0, keepdims=True)
        window_start = window_start + advance
    errors = jnp.stack(error_rows).reshape(ROUNDS, ITERS, 1)
    return (current, errors)


def solution(mesh):
    split = Mesh(
        mesh.devices.reshape(mesh.shape["groups"], 8, 8, 2),
        ("groups", "steps_0", "steps_1", "steps_2"),
    )
    in_specs = (P(GROUPS_STEPS, None, None), P("groups"), P("groups"), P(), P(), P(), P())
    out_specs = (P(GROUPS_STEPS, None, None), P("groups", None, STEPS))
    return jax.shard_map(
        shards, mesh=split, in_specs=in_specs, out_specs=out_specs, check_vma=False
    )
```

profile of v0, /device:TPU:513, one launch (start us, length us, event | category | flops | bytes accessed | tf_op | source)
XLA Modules:
  0.0 739.3 jit_solution(762342680965915315)
XLA Ops:
  30.4 22.0 %all-gather = f32[2,4,4096]{2,1,0:T(4,128)S(1)} all-gather(f32[1,4,4096]{2,1,0:T(4,128)S(1)} %fusion.34), channel_id=2, replica_groups=mesh['groups'=2,'steps_0'=8,'steps_1'=8,'steps_2'=2] {'steps_2'}, dimensions={0}, use_global_device_ids=true | all-gather | bytes 196608 | tf_op jit(solution)/shard_map/all_gather | solution.py:24
  52.5 19.3 %all-gather.8 = f32[8,4,4096]{2,1,0:T(4,128)S(1)} all-gather(f32[1,4,4096]{2,1,0:T(4,128)S(1)} %slice_add_fusion.95), channel_id=10, replica_groups=mesh['groups'=2,'steps_0'=8,'steps_1'=8,'steps_2'=2] {'steps_1'}, dimensions={0}, use_global_device_ids=true | all-gather | bytes 589824 | tf_op jit(solution)/shard_map/all_gather | solution.py:24
  71.8 19.8 %all_gather.121 = f32[8,1,4,4096]{3,2,1,0:T(4,128)S(1)} all-gather(f32[1,1,4,4096]{3,2,1,0:T(4,128)S(1)} %get-tuple-element.42), channel_id=1, replica_groups=mesh['groups'=2,'steps_0'=8,'steps_1'=8,'steps_2'=2] {'steps_0'}, dimensions={0}, use_global_device_ids=true | all-gather | bytes 589824 | tf_op jit(solution)/shard_map/all_gather | solution.py:24
  102.6 13.6 %all-gather.1 = f32[2,4,4096]{2,1,0:T(4,128)S(1)} all-gather(f32[1,4,4096]{2,1,0:T(4,128)S(1)} %fusion.31), channel_id=3, replica_groups=mesh['groups'=2,'steps_0'=8,'steps_1'=8,'steps_2'=2] {'steps_2'}, dimensions={0}, use_global_device_ids=true | all-gather | bytes 196608 | tf_op jit(solution)/shard_map/all_gather | solution.py:24
  116.3 19.3 %all-gather.9 = f32[8,4,4096]{2,1,0:T(4,128)S(1)} all-gather(f32[1,4,4096]{2,1,0:T(4,128)S(1)} %slice_add_fusion.82), channel_id=11, replica_groups=mesh['groups'=2,'steps_0'=8,'steps_1'=8,'steps_2'=2] {'steps_1'}, dimensions={0}, use_global_device_ids=true | all-gather | bytes 589824 | tf_op jit(solution)/shard_map/all_gather | solution.py:24
  135.6 19.3 %all_gather.125 = f32[8,1,4,4096]{3,2,1,0:T(4,128)S(1)} all-gather(f32[1,1,4,4096]{3,2,1,0:T(4,128)S(1)} %get-tuple-element.40), channel_id=1, replica_groups=mesh['groups'=2,'steps_0'=8,'steps_1'=8,'steps_2'=2] {'steps_0'}, dimensions={0}, use_global_device_ids=true | all-gather | bytes 589824 | tf_op jit(solution)/shard_map/all_gather | solution.py:24
  165.8 14.0 %all-gather.2 = f32[2,4,4096]{2,1,0:T(4,128)S(1)} all-gather(f32[1,4,4096]{2,1,0:T(4,128)S(1)} %fusion.28), channel_id=4, replica_groups=mesh['groups'=2,'steps_0'=8,'steps_1'=8,'steps_2'=2] {'steps_2'}, dimensions={0}, use_global_device_ids=true | all-gather | bytes 196608 | tf_op jit(solution)/shard_map/all_gather | solution.py:24
  179.9 19.3 %all-gather.10 = f32[8,4,4096]{2,1,0:T(4,128)S(1)} all-gather(f32[1,4,4096]{2,1,0:T(4,128)S(1)} %slice_add_fusion.69), channel_id=12, replica_groups=mesh['groups'=2,'steps_0'=8,'steps_1'=8,'steps_2'=2] {'steps_1'}, dimensions={0}, use_global_device_ids=true | all-gather | bytes 589824 | tf_op jit(solution)/shard_map/all_gather | solution.py:24
  199.3 19.5 %all_gather.129 = f32[8,1,4,4096]{3,2,1,0:T(4,128)S(1)} all-gather(f32[1,1,4,4096]{3,2,1,0:T(4,128)S(1)} %get-tuple-element.38), channel_id=1, replica_groups=mesh['groups'=2,'steps_0'=8,'steps_1'=8,'steps_2'=2] {'steps_0'}, dimensions={0}, use_global_device_ids=true | all-gather | bytes 589824 | tf_op jit(solution)/shard_map/all_gather | solution.py:24
  229.7 14.0 %all-gather.3 = f32[2,4,4096]{2,1,0:T(4,128)S(1)} all-gather(f32[1,4,4096]{2,1,0:T(4,128)S(1)} %fusion.25), channel_id=5, replica_groups=mesh['groups'=2,'steps_0'=8,'steps_1'=8,'steps_2'=2] {'steps_2'}, dimensions={0}, use_global_device_ids=true | all-gather | bytes 196608 | tf_op jit(solution)/shard_map/all_gather | solution.py:24
  243.7 19.6 %all-gather.11 = f32[8,4,4096]{2,1,0:T(4,128)S(1)} all-gather(f32[1,4,4096]{2,1,0:T(4,128)S(1)} %slice_add_fusion.56), channel_id=13, replica_groups=mesh['groups'=2,'steps_0'=8,'steps_1'=8,'steps_2'=2] {'steps_1'}, dimensions={0}, use_global_device_ids=true | all-gather | bytes 589824 | tf_op jit(solution)/shard_map/all_gather | solution.py:24
  263.4 19.5 %all_gather.133 = f32[8,1,4,4096]{3,2,1,0:T(4,128)S(1)} all-gather(f32[1,1,4,4096]{3,2,1,0:T(4,128)S(1)} %get-tuple-element.36), channel_id=1, replica_groups=mesh['groups'=2,'steps_0'=8,'steps_1'=8,'steps_2'=2] {'steps_0'}, dimensions={0}, use_global_device_ids=true | all-gather | bytes 589824 | tf_op jit(solution)/shard_map/all_gather | solution.py:24
  288.8 91.7 %all-gather.27.cloned.1.call-done = f32[128,4,4096]{2,1,0:T(4,128)} async-done(((f32[1,4,4096]{2,1,0:T(4,128)}), f32[128,4,4096]{2,1,0:T(4,128)}) %all-gather.27.cloned.1.call-update) | async-done | bytes 8388624 | tf_op jit(solution)/shard_map/all_gather | solution.py:99
  399.1 19.9 %all-gather.17 = f32[8,4,4096]{2,1,0:T(4,128)S(1)} all-gather(f32[1,4,4096]{2,1,0:T(4,128)S(1)} %slice_add_fusion.43), channel_id=14, replica_groups=mesh['groups'=2,'steps_0'=8,'steps_1'=8,'steps_2'=2] {'steps_1'}, dimensions={0}, use_global_device_ids=true | all-gather | bytes 589824 | tf_op jit(solution)/shard_map/all_gather | solution.py:24
  419.0 20.6 %all_gather.138 = f32[8,1,4,4096]{3,2,1,0:T(4,128)S(1)} all-gather(f32[1,1,4,4096]{3,2,1,0:T(4,128)S(1)} %get-tuple-element.34), channel_id=1, replica_groups=mesh['groups'=2,'steps_0'=8,'steps_1'=8,'steps_2'=2] {'steps_0'}, dimensions={0}, use_global_device_ids=true | all-gather | bytes 589824 | tf_op jit(solution)/shard_map/all_gather | solution.py:24
  463.2 19.3 %all-gather.19 = f32[8,4,4096]{2,1,0:T(4,128)S(1)} all-gather(f32[1,4,4096]{2,1,0:T(4,128)S(1)} %slice_add_fusion.32), channel_id=15, replica_groups=mesh['groups'=2,'steps_0'=8,'steps_1'=8,'steps_2'=2] {'steps_1'}, dimensions={0}, use_global_device_ids=true | all-gather | bytes 589824 | tf_op jit(solution)/shard_map/all_gather | solution.py:24
  482.6 19.4 %all_gather.142 = f32[8,1,4,4096]{3,2,1,0:T(4,128)S(1)} all-gather(f32[1,1,4,4096]{3,2,1,0:T(4,128)S(1)} %get-tuple-element.30), channel_id=1, replica_groups=mesh['groups'=2,'steps_0'=8,'steps_1'=8,'steps_2'=2] {'steps_0'}, dimensions={0}, use_global_device_ids=true | all-gather | bytes 589824 | tf_op jit(solution)/shard_map/all_gather | solution.py:24
  513.0 14.3 %all-gather.20 = f32[2,4,4096]{2,1,0:T(4,128)S(1)} all-gather(f32[1,4,4096]{2,1,0:T(4,128)S(1)} %fusion.14), channel_id=8, replica_groups=mesh['groups'=2,'steps_0'=8,'steps_1'=8,'steps_2'=2] {'steps_2'}, dimensions={0}, use_global_device_ids=true | all-gather | bytes 196608 | tf_op jit(solution)/shard_map/all_gather | solution.py:24
  527.3 20.1 %all-gather.21 = f32[8,4,4096]{2,1,0:T(4,128)S(1)} all-gather(f32[1,4,4096]{2,1,0:T(4,128)S(1)} %slice_add_fusion.21), channel_id=16, replica_groups=mesh['groups'=2,'steps_0'=8,'steps_1'=8,'steps_2'=2] {'steps_1'}, dimensions={0}, use_global_device_ids=true | all-gather | bytes 589824 | tf_op jit(solution)/shard_map/all_gather | solution.py:24
  547.4 19.4 %all_gather.146 = f32[8,1,4,4096]{3,2,1,0:T(4,128)S(1)} all-gather(f32[1,1,4,4096]{3,2,1,0:T(4,128)S(1)} %get-tuple-element.26), channel_id=1, replica_groups=mesh['groups'=2,'steps_0'=8,'steps_1'=8,'steps_2'=2] {'steps_0'}, dimensions={0}, use_global_device_ids=true | all-gather | bytes 589824 | tf_op jit(solution)/shard_map/all_gather | solution.py:24
  577.7 13.6 %all-gather.22 = f32[2,4,4096]{2,1,0:T(4,128)S(1)} all-gather(f32[1,4,4096]{2,1,0:T(4,128)S(1)} %fusion.10), channel_id=9, replica_groups=mesh['groups'=2,'steps_0'=8,'steps_1'=8,'steps_2'=2] {'steps_2'}, dimensions={0}, use_global_device_ids=true | all-gather | bytes 196608 | tf_op jit(solution)/shard_map/all_gather | solution.py:24
  591.3 19.9 %all-gather.23 = f32[8,4,4096]{2,1,0:T(4,128)S(1)} all-gather(f32[1,4,4096]{2,1,0:T(4,128)S(1)} %slice_add_fusion.10), channel_id=17, replica_groups=mesh['groups'=2,'steps_0'=8,'steps_1'=8,'steps_2'=2] {'steps_1'}, dimensions={0}, use_global_device_ids=true | all-gather | bytes 589824 | tf_op jit(solution)/shard_map/all_gather | solution.py:24
  611.3 19.3 %all_gather.150 = f32[8,1,4,4096]{3,2,1,0:T(4,128)S(1)} all-gather(f32[1,1,4,4096]{3,2,1,0:T(4,128)S(1)} %get-tuple-element.22), channel_id=1, replica_groups=mesh['groups'=2,'steps_0'=8,'steps_1'=8,'steps_2'=2] {'steps_0'}, dimensions={0}, use_global_device_ids=true | all-gather | bytes 589824 | tf_op jit(solution)/shard_map/all_gather | solution.py:24
  638.5 87.3 %all-gather.29.cloned.1.call-done = f32[128,4,4096]{2,1,0:T(4,128)} async-done(((f32[1,4,4096]{2,1,0:T(4,128)}), f32[128,4,4096]{2,1,0:T(4,128)}) %all-gather.29.cloned.1.call-update) | async-done | bytes 8388624 | tf_op jit(solution)/shard_map/all_gather | solution.py:99
  (84 shorter events, 127.8 us)
Async XLA Ops:
  7.2 11.0 %copy-start = (f32[320,320]{1,0:T(8,128)S(1)}, f32[320,320]{1,0:T(8,128)}, u32[]{:S(2)}) copy-start(f32[320,320]{1,0:T(8,128)} %param.11) | copy-start | bytes 1228804
  7.2 15.7 %copy-start.2 = (f32[1,4,4096]{2,1,0:T(4,128)S(1)}, f32[1,4,4096]{2,1,0:T(4,128)}, u32[]{:S(2)}) copy-start(f32[1,4,4096]{2,1,0:T(4,128)} %param.7) | copy-start | bytes 196612
  7.2 15.7 %copy-start.4 = (bf16[320,320]{1,0:T(8,128)(2,1)S(1)}, bf16[320,320]{1,0:T(8,128)(2,1)}, u32[]{:S(2)}) copy-start(bf16[320,320]{1,0:T(8,128)(2,1)} %param.12) | copy-start | bytes 614404
  7.2 15.7 %copy-start.5 = (bf16[4,320]{1,0:T(4,128)(2,1)S(1)}, bf16[4,320]{1,0:T(4,128)(2,1)}, u32[]{:S(2)}) copy-start(bf16[4,320]{1,0:T(4,128)(2,1)} %param.13) | copy-start | bytes 7684
  7.2 373.3 %all-gather.27.cloned.1.call-start = ((), (), s32[]{:S(2)}) async-start(), calls=%async_computation | async-start | bytes 8454144 | tf_op jit(solution)/shard_map/all_gather | solution.py:99
  22.9 69.0 %copy-start.3 = (bf16[320,4]{0,1:T(4,128)(2,1)S(1)}, bf16[320,4]{0,1:T(4,128)(2,1)}, u32[]{:S(2)}) copy-start(bf16[320,4]{0,1:T(4,128)(2,1)} %param.10) | copy-start | bytes 7684
  284.4 441.4 %all-gather.29.cloned.1.call-start = ((), (), s32[]{:S(2)}) async-start(), calls=%async_computation.1 | async-start | bytes 8454144 | tf_op jit(solution)/shard_map/all_gather | solution.py:99
  630.6 101.7 %copy-start.1 = (f32[320,320]{1,0:T(8,128)S(1)}, f32[320,320]{1,0:T(8,128)}, u32[]{:S(2)}) copy-start(f32[320,320]{1,0:T(8,128)} %param.11) | copy-start | bytes 1228804
Sparse Core Ops, SparseCore 0:
  284.6 95.8 all-gather.26
  632.4 93.3 all-gather.28
where the time goes:
time: 748 us; the launch traced here: 739 us
  blocking collectives  420 us (56%)
  waiting for transfers between devices  179 us (24%)
  matrix products  88 us (12%)
  between operations  27.5 us (4%)
  other arithmetic  21.6 us (3%)
    all_gather x24, blocking collectives, entering(): pieces = lax.all_gather(so_far, axis)  420 us
    all_gather x2, waiting for transfers between devices, shards(): block = lax.all_gather(current, STEPS, axis=0, tiled=True)  179 us
    dot_general x8, matrix products, denoise(): return jnp.dot(out_weight, hidden_two, preferred_element_type=jnp.float32)  60.3 us
    dot_general x8, matrix products, denoise(): jnp.dot(in_weight, state.astype(jnp.bfloat16), preferred_element_type=jnp...  26.6 us
  transfers between devices with their start and end apart: 2, of which 2 were waited for; matrix products, arithmetic and copies ran while one was open for 0% of the time, Pallas kernels for 0%

commit v1 on v0

--- a/solution.py
+++ b/solution.py
@@ -96,7 +96,9 @@
         advance = advances[round_no]
         target = own_index + advance
         wanted = jnp.minimum(target, window - 1)
-        block = lax.all_gather(current, STEPS, axis=0, tiled=True)
+        block = jnp.concatenate(
+            lax.all_to_all(jnp.stack([current] * lax.axis_size(STEPS)), STEPS, 0, 0), axis=0
+        )
         row_ids = jnp.arange(block.shape[0], dtype=jnp.int32)
         selected = jnp.where((row_ids == wanted)[:, None, None], block, 0.0)
         current = jnp.zeros_like(current) + jnp.sum(selected, axis=0, keepdims=True)

time: 748 us -> 1080 us (1.44)
  the two profiles are of different devices: /device:TPU:513 before, /device:TPU:553 now
where the time goes in v1:
time: 1080 us
  waiting for transfers between devices  472 us (44%)
  blocking collectives  413 us (38%)
  matrix products  88 us (8%)
  starting transfers between devices  53.9 us (5%)
  other arithmetic  20.5 us (2%)
  between operations  14.3 us (1%)
  local copies, waits for them, and re-layouts  13.7 us (1%)
    all_to_all x2, waiting for transfers between devices, shards(): lax.all_to_all(jnp.stack([current] * lax.axis_size(STEPS)), STEPS, 0, 0)  472 us
    all_gather x24, blocking collectives, entering(): pieces = lax.all_gather(so_far, axis)  413 us
    dot_general x8, matrix products, denoise(): return jnp.dot(out_weight, hidden_two, preferred_element_type=jnp.float32)  60.3 us
    all_to_all x2, starting transfers between devices, shards(): lax.all_to_all(jnp.stack([current] * lax.axis_size(STEPS)), STEPS, 0, 0)  53.9 us
    dot_general x8, matrix products, denoise(): jnp.dot(in_weight, state.astype(jnp.bfloat16), preferred_element_type=jnp...  26.6 us
  transfers between devices with their start and end apart: 2, of which 2 were waited for; matrix products, arithmetic and copies ran while one was open for 0% of the time, Pallas kernels for 0%

profile of v1, /device:TPU:553, one launch (start us, length us, event | category | flops | bytes accessed | tf_op | source)
XLA Modules:
  0.0 1075.5 jit_solution(3037626748209976962)
XLA Ops:
  26.1 19.4 %all-gather.8 = f32[8,4,4096]{2,1,0:T(4,128)S(1)} all-gather(f32[1,4,4096]{2,1,0:T(4,128)S(1)} %slice_add_fusion.95), channel_id=10, replica_groups=mesh['groups'=2,'steps_0'=8,'steps_1'=8,'steps_2'=2] {'steps_1'}, dimensions={0}, use_global_device_ids=true | all-gather | bytes 589824 | tf_op jit(solution)/shard_map/all_gather | solution.py:24
  45.6 29.1 %all_gather.115 = f32[8,1,4,4096]{3,2,1,0:T(4,128)S(1)} all-gather(f32[1,1,4,4096]{3,2,1,0:T(4,128)S(1)} %get-tuple-element.42), channel_id=1, replica_groups=mesh['groups'=2,'steps_0'=8,'steps_1'=8,'steps_2'=2] {'steps_0'}, dimensions={0}, use_global_device_ids=true | all-gather | bytes 589824 | tf_op jit(solution)/shard_map/all_gather | solution.py:24
  85.6 13.5 %all-gather.1 = f32[2,4,4096]{2,1,0:T(4,128)S(1)} all-gather(f32[1,4,4096]{2,1,0:T(4,128)S(1)} %fusion.33), channel_id=3, replica_groups=mesh['groups'=2,'steps_0'=8,'steps_1'=8,'steps_2'=2] {'steps_2'}, dimensions={0}, use_global_device_ids=true | all-gather | bytes 196608 | tf_op jit(solution)/shard_map/all_gather | solution.py:24
  99.2 20.1 %all-gather.9 = f32[8,4,4096]{2,1,0:T(4,128)S(1)} all-gather(f32[1,4,4096]{2,1,0:T(4,128)S(1)} %slice_add_fusion.82), channel_id=11, replica_groups=mesh['groups'=2,'steps_0'=8,'steps_1'=8,'steps_2'=2] {'steps_1'}, dimensions={0}, use_global_device_ids=true | all-gather | bytes 589824 | tf_op jit(solution)/shard_map/all_gather | solution.py:24
  119.3 19.8 %all_gather.119 = f32[8,1,4,4096]{3,2,1,0:T(4,128)S(1)} all-gather(f32[1,1,4,4096]{3,2,1,0:T(4,128)S(1)} %get-tuple-element.40), channel_id=1, replica_groups=mesh['groups'=2,'steps_0'=8,'steps_1'=8,'steps_2'=2] {'steps_0'}, dimensions={0}, use_global_device_ids=true | all-gather | bytes 589824 | tf_op jit(solution)/shard_map/all_gather | solution.py:24
  163.1 19.8 %all-gather.10 = f32[8,4,4096]{2,1,0:T(4,128)S(1)} all-gather(f32[1,4,4096]{2,1,0:T(4,128)S(1)} %slice_add_fusion.69), channel_id=12, replica_groups=mesh['groups'=2,'steps_0'=8,'steps_1'=8,'steps_2'=2] {'steps_1'}, dimensions={0}, use_global_device_ids=true | all-gather | bytes 589824 | tf_op jit(solution)/shard_map/all_gather | solution.py:24
  183.0 20.3 %all_gather.123 = f32[8,1,4,4096]{3,2,1,0:T(4,128)S(1)} all-gather(f32[1,1,4,4096]{3,2,1,0:T(4,128)S(1)} %get-tuple-element.38), channel_id=1, replica_groups=mesh['groups'=2,'steps_0'=8,'steps_1'=8,'steps_2'=2] {'steps_0'}, dimensions={0}, use_global_device_ids=true | all-gather | bytes 589824 | tf_op jit(solution)/shard_map/all_gather | solution.py:24
  227.5 19.8 %all-gather.11 = f32[8,4,4096]{2,1,0:T(4,128)S(1)} all-gather(f32[1,4,4096]{2,1,0:T(4,128)S(1)} %slice_add_fusion.56), channel_id=13, replica_groups=mesh['groups'=2,'steps_0'=8,'steps_1'=8,'steps_2'=2] {'steps_1'}, dimensions={0}, use_global_device_ids=true | all-gather | bytes 589824 | tf_op jit(solution)/shard_map/all_gather | solution.py:24
  247.3 19.8 %all_gather.127 = f32[8,1,4,4096]{3,2,1,0:T(4,128)S(1)} all-gather(f32[1,1,4,4096]{3,2,1,0:T(4,128)S(1)} %get-tuple-element.36), channel_id=1, replica_groups=mesh['groups'=2,'steps_0'=8,'steps_1'=8,'steps_2'=2] {'steps_0'}, dimensions={0}, use_global_device_ids=true | all-gather | bytes 589824 | tf_op jit(solution)/shard_map/all_gather | solution.py:24
  273.4 26.5 %all-to-all-start = ((f32[128,1,4,4096]{3,2,1,0:T(4,128)}), f32[128,1,4,4096]{3,2,1,0:T(4,128)}, u32[]{:S(2)}, u32[]{:S(2)}) async-start(f32[128,1,4,4096]{3,2,1,0:T(4,128)} %stack.32), calls=%async_computation | async-start | bytes 16777216 | tf_op jit(solution)/shard_map/all_to_all | solution.py:100
  303.9 231.9 %all-to-all-done = f32[128,1,4,4096]{3,2,1,0:T(4,128)} async-done(((f32[128,1,4,4096]{3,2,1,0:T(4,128)}), f32[128,1,4,4096]{3,2,1,0:T(4,128)}, u32[]{:S(2)}, u32[]{:S(2)}) %all-to-all-start) | async-done | bytes 8388640 | tf_op jit(solution)/shard_map/all_to_all | solution.py:100
  554.3 19.4 %all-gather.17 = f32[8,4,4096]{2,1,0:T(4,128)S(1)} all-gather(f32[1,4,4096]{2,1,0:T(4,128)S(1)} %slice_add_fusion.43), channel_id=14, replica_groups=mesh['groups'=2,'steps_0'=8,'steps_1'=8,'steps_2'=2] {'steps_1'}, dimensions={0}, use_global_device_ids=true | all-gather | bytes 589824 | tf_op jit(solution)/shard_map/all_gather | solution.py:24
  573.8 23.4 %all_gather.131 = f32[8,1,4,4096]{3,2,1,0:T(4,128)S(1)} all-gather(f32[1,1,4,4096]{3,2,1,0:T(4,128)S(1)} %get-tuple-element.34), channel_id=1, replica_groups=mesh['groups'=2,'steps_0'=8,'steps_1'=8,'steps_2'=2] {'steps_0'}, dimensions={0}, use_global_device_ids=true | all-gather | bytes 589824 | tf_op jit(solution)/shard_map/all_gather | solution.py:24
  608.1 14.2 %all-gather.18 = f32[2,4,4096]{2,1,0:T(4,128)S(1)} all-gather(f32[1,4,4096]{2,1,0:T(4,128)S(1)} %fusion.20), channel_id=7, replica_groups=mesh['groups'=2,'steps_0'=8,'steps_1'=8,'steps_2'=2] {'steps_2'}, dimensions={0}, use_global_device_ids=true | all-gather | bytes 196608 | tf_op jit(solution)/shard_map/all_gather | solution.py:24
  622.2 19.8 %all-gather.19 = f32[8,4,4096]{2,1,0:T(4,128)S(1)} all-gather(f32[1,4,4096]{2,1,0:T(4,128)S(1)} %slice_add_fusion.32), channel_id=15, replica_groups=mesh['groups'=2,'steps_0'=8,'steps_1'=8,'steps_2'=2] {'steps_1'}, dimensions={0}, use_global_device_ids=true | all-gather | bytes 589824 | tf_op jit(solution)/shard_map/all_gather | solution.py:24
  642.1 18.9 %all_gather.135 = f32[8,1,4,4096]{3,2,1,0:T(4,128)S(1)} all-gather(f32[1,1,4,4096]{3,2,1,0:T(4,128)S(1)} %get-tuple-element.30), channel_id=1, replica_groups=mesh['groups'=2,'steps_0'=8,'steps_1'=8,'steps_2'=2] {'steps_0'}, dimensions={0}, use_global_device_ids=true | all-gather | bytes 589824 | tf_op jit(solution)/shard_map/all_gather | solution.py:24
  672.0 14.0 %all-gather.20 = f32[2,4,4096]{2,1,0:T(4,128)S(1)} all-gather(f32[1,4,4096]{2,1,0:T(4,128)S(1)} %fusion.16), channel_id=8, replica_groups=mesh['groups'=2,'steps_0'=8,'steps_1'=8,'steps_2'=2] {'steps_2'}, dimensions={0}, use_global_device_ids=true | all-gather | bytes 196608 | tf_op jit(solution)/shard_map/all_gather | solution.py:24
  686.0 19.9 %all-gather.21 = f32[8,4,4096]{2,1,0:T(4,128)S(1)} all-gather(f32[1,4,4096]{2,1,0:T(4,128)S(1)} %slice_add_fusion.21), channel_id=16, replica_groups=mesh['groups'=2,'steps_0'=8,'steps_1'=8,'steps_2'=2] {'steps_1'}, dimensions={0}, use_global_device_ids=true | all-gather | bytes 589824 | tf_op jit(solution)/shard_map/all_gather | solution.py:24
  705.9 19.1 %all_gather.139 = f32[8,1,4,4096]{3,2,1,0:T(4,128)S(1)} all-gather(f32[1,1,4,4096]{3,2,1,0:T(4,128)S(1)} %get-tuple-element.26), channel_id=1, replica_groups=mesh['groups'=2,'steps_0'=8,'steps_1'=8,'steps_2'=2] {'steps_0'}, dimensions={0}, use_global_device_ids=true | all-gather | bytes 589824 | tf_op jit(solution)/shard_map/all_gather | solution.py:24
  735.9 14.1 %all-gather.22 = f32[2,4,4096]{2,1,0:T(4,128)S(1)} all-gather(f32[1,4,4096]{2,1,0:T(4,128)S(1)} %fusion.12), channel_id=9, replica_groups=mesh['groups'=2,'steps_0'=8,'steps_1'=8,'steps_2'=2] {'steps_2'}, dimensions={0}, use_global_device_ids=true | all-gather | bytes 196608 | tf_op jit(solution)/shard_map/all_gather | solution.py:24
  750.0 19.4 %all-gather.23 = f32[8,4,4096]{2,1,0:T(4,128)S(1)} all-gather(f32[1,4,4096]{2,1,0:T(4,128)S(1)} %slice_add_fusion.10), channel_id=17, replica_groups=mesh['groups'=2,'steps_0'=8,'steps_1'=8,'steps_2'=2] {'steps_1'}, dimensions={0}, use_global_device_ids=true | all-gather | bytes 589824 | tf_op jit(solution)/shard_map/all_gather | solution.py:24
  769.5 19.3 %all_gather.143 = f32[8,1,4,4096]{3,2,1,0:T(4,128)S(1)} all-gather(f32[1,1,4,4096]{3,2,1,0:T(4,128)S(1)} %get-tuple-element.22), channel_id=1, replica_groups=mesh['groups'=2,'steps_0'=8,'steps_1'=8,'steps_2'=2] {'steps_0'}, dimensions={0}, use_global_device_ids=true | all-gather | bytes 589824 | tf_op jit(solution)/shard_map/all_gather | solution.py:24
  794.9 27.4 %all-to-all-start.1 = ((f32[128,1,4,4096]{3,2,1,0:T(4,128)}), f32[128,1,4,4096]{3,2,1,0:T(4,128)}, u32[]{:S(2)}, u32[]{:S(2)}) async-start(f32[128,1,4,4096]{3,2,1,0:T(4,128)} %stack.34), calls=%async_computation.1 | async-start | bytes 16777216 | tf_op jit(solution)/shard_map/all_to_all | solution.py:100
  828.9 239.9 %all-to-all-done.1 = f32[128,1,4,4096]{3,2,1,0:T(4,128)} async-done(((f32[128,1,4,4096]{3,2,1,0:T(4,128)}), f32[128,1,4,4096]{3,2,1,0:T(4,128)}, u32[]{:S(2)}, u32[]{:S(2)}) %all-to-all-start.1) | async-done | bytes 8388640 | tf_op jit(solution)/shard_map/all_to_all | solution.py:100
  (84 shorter events, 152.6 us)
Async XLA Ops:
  0.6 11.0 %copy-start = (f32[320,320]{1,0:T(8,128)S(1)}, f32[320,320]{1,0:T(8,128)}, u32[]{:S(2)}) copy-start(f32[320,320]{1,0:T(8,128)} %param.11) | copy-start | bytes 1228804
  0.6 15.7 %copy-start.2 = (f32[1,4,4096]{2,1,0:T(4,128)S(1)}, f32[1,4,4096]{2,1,0:T(4,128)}, u32[]{:S(2)}) copy-start(f32[1,4,4096]{2,1,0:T(4,128)} %param.7) | copy-start | bytes 196612
  0.7 15.7 %copy-start.4 = (bf16[320,320]{1,0:T(8,128)(2,1)S(1)}, bf16[320,320]{1,0:T(8,128)(2,1)}, u32[]{:S(2)}) copy-start(bf16[320,320]{1,0:T(8,128)(2,1)} %param.12) | copy-start | bytes 614404
  0.7 15.7 %copy-start.5 = (bf16[4,320]{1,0:T(4,128)(2,1)S(1)}, bf16[4,320]{1,0:T(4,128)(2,1)}, u32[]{:S(2)}) copy-start(bf16[4,320]{1,0:T(4,128)(2,1)} %param.13) | copy-start | bytes 7684
  16.3 58.5 %copy-start.3 = (bf16[320,4]{0,1:T(4,128)(2,1)S(1)}, bf16[320,4]{0,1:T(4,128)(2,1)}, u32[]{:S(2)}) copy-start(bf16[320,4]{0,1:T(4,128)(2,1)} %param.10) | copy-start | bytes 7684
  273.4 262.4 %all-to-all-start = ((f32[128,1,4,4096]{3,2,1,0:T(4,128)}), f32[128,1,4,4096]{3,2,1,0:T(4,128)}, u32[]{:S(2)}, u32[]{:S(2)}) async-start(f32[128,1,4,4096]{3,2,1,0:T(4,128)} %stack.32), calls=%async_computation | async-start | bytes 16777216 | tf_op jit(solution)/shard_map/all_to_all | solution.py:100
  794.9 273.9 %all-to-all-start.1 = ((f32[128,1,4,4096]{3,2,1,0:T(4,128)}), f32[128,1,4,4096]{3,2,1,0:T(4,128)}, u32[]{:S(2)}, u32[]{:S(2)}) async-start(f32[128,1,4,4096]{3,2,1,0:T(4,128)} %stack.34), calls=%async_computation.1 | async-start | bytes 16777216 | tf_op jit(solution)/shard_map/all_to_all | solution.py:100
  822.4 253.0 %copy-start.1 = (f32[320,320]{1,0:T(8,128)S(1)}, f32[320,320]{1,0:T(8,128)}, u32[]{:S(2)}) copy-start(f32[320,320]{1,0:T(8,128)} %param.11) | copy-start | bytes 1228804
